TPU v7x, 32 devices: a whole 2x2x4 slice. The times are simulated.
32 devices in a mesh: groups: 2 (over y), assets: 8 (over z, x), tm: 2 (over core).
Axes of the slice: x: 2, y: 2, z: 4, core: 2. Of those that a mesh axis runs over, the one named last changes fastest.
Arguments:
- returns: bfloat16 [1536, 16384], P('tm', ('groups', 'assets')), parts along dimension 1, may hold values from -24 to 24
- prior: float32 [16384, 8192], P(('groups', 'assets')), parts along dimension 0, may hold values from -3 to 3
Outputs:
- covariance: float32 [2, 16384, 8192], P('tm', ('groups', 'assets')), parts along dimension 1
There are 2 independent parts, one for each index of `groups`. A program takes and returns all parts, laid end to end along the dimension named above; each array names one. Nothing has to cross between parts.
All inputs are finite; a program needn't handle non-finite values.
Results may differ from a plain program's by a relative error of at most 0.0045.
Values may be sent and summed in bfloat16 or wider, within the bound.
A program may use at most 256 MiB of HBM per device.

v0:
```python
import jax
import jax.numpy as jnp
from jax import lax
from jax.sharding import PartitionSpec as P


def prefix(shard, axis, combine, identity):
    length, mine = (lax.axis_size(axis), lax.axis_index(axis))
    everything = jax.tree.map(
        lambda part, kind: lax.all_gather(part.astype(kind), axis),
        shard,
        (jnp.bfloat16, jnp.bfloat16),
    )
    start = jax.tree.map(
        lambda part, zero: jnp.broadcast_to(jnp.asarray(zero, part.dtype), part.shape),
        shard,
        identity,
    )

    def turn(k, before):
        reached = k < mine
        new = combine(
            before, jax.tree.map(lambda part, own: part[k].astype(own.dtype), everything, shard)
        )
        return jax.tree.map(lambda a, b: jnp.where(reached, a, b), new, before)

    return lax.fori_loop(0, length, turn, start)


def cross_tile(left, right):
    return lax.dot_general(
        left, right, (((0,), (0,)), ((), ())), preferred_element_type=jnp.float32
    )


def combine_carry(earlier, later):
    return (later[1] * earlier[0] + later[0], earlier[1] * later[1])


def local(returns, prior):
    minutes, width = returns.shape
    lam = jnp.float32(0.9995)
    position = jnp.arange(minutes, dtype=jnp.float32)
    weight = jnp.sqrt(
        (jnp.float32(1.0) - lam) * jnp.power(lam, jnp.float32(minutes - 1) - position)
    )
    factor = jnp.power(lam, jnp.float32(minutes))
    scaled = (returns.astype(jnp.float32) * weight[:, None]).astype(jnp.bfloat16)
    tile = cross_tile(scaled, lax.all_gather(scaled, "assets", axis=1, tiled=True))
    decay = jnp.full((1,), factor, jnp.float32)
    identity = (jnp.zeros_like(tile), jnp.ones((1,), jnp.float32))
    before, reach = prefix((tile, decay), "tm", combine_carry, identity)
    result = factor * (before + reach[0] * prior) + tile
    return result[None]


def solution(mesh):
    placed = (P("tm", ("groups", "assets")), P(("groups", "assets"), None))
    return jax.shard_map(
        local,
        mesh=mesh,
        in_specs=placed,
        out_specs=P("tm", ("groups", "assets"), None),
        check_vma=False,
    )
```

profile of v0, /device:TPU:0, one launch (start us, length us, event | category | flops | bytes accessed | tf_op | source)
XLA Modules:
  0.0 360.6 jit_solution(16871190527637498569)
XLA Ops:
  6.5 0.0 all-gather.4.cloned.1.call-start
  6.6 2.9 multiply_convert_fusion
  9.5 0.0 all-gather.4.cloned.1.call-update
  9.5 0.0 copy-start
  9.5 0.0 all-gather.6.cloned.1.call-start
  9.6 178.9 %all-gather.4.cloned.1.call-done = bf16[768,8192]{1,0:T(8,128)(2,1)} async-done(((bf16[768,1024]{1,0:T(8,128)(2,1)}), bf16[768,8192]{1,0:T(8,128)(2,1)}) %all-gather.4.cloned.1.call-update) | async-done | bytes 12582928 | tf_op jit(solution)/shard_map/all_gather | solution.py:49
  188.5 24.6 %fusion.1 = (bf16[1024,8192]{1,0:T(8,128)(2,1)}, f32[1024,8192]{1,0:T(8,128)}) fusion(bf16[768,1024]{1,0:T(8,128)(2,1)} %multiply_convert_fusion, bf16[768,8192]{1,0:T(8,128)(2,1)} %all-gather.4.cloned.1.call-done), kind=kOutput, calls=%fused_computation.6 | convolution fusion | flops 12893290496 | bytes 64487424 | tf_op jit(solution)/shard_map/dot_general | solution.py:31
  213.1 0.0 all-gather.6.cloned.1.call-update
  213.1 0.0 copy-done
  213.1 0.6 dynamic-slice
  213.7 0.7 dynamic-update-slice
  214.4 2.4 all-reduce
  216.9 45.6 %all-gather.6.cloned.1.call-done = bf16[2048,8192]{1,0:T(8,128)(2,1)} async-done(((bf16[1024,8192]{1,0:T(8,128)(2,1)}), bf16[2048,8192]{1,0:T(8,128)(2,1)}) %all-gather.6.cloned.1.call-update) | async-done | bytes 33554448 | tf_op jit(solution)/shard_map/all_gather | solution.py:10
  262.4 48.2 %while.16 = (s32[]{:T(128)}, f32[1024,8192]{1,0:T(8,128)}, f32[1]{0:T(128)}, s32[]{:T(128)}, bf16[2,1]{0,1:T(2,128)(2,1)S(1)}, /*index=5*/bf16[2,1024,8192]{2,1,0:T(8,128)(2,1)}, s32[]{:T(128)}, s32[]{:T(128)}) while((s32[]{:T(128)}, f32[1024,8192]{1,0:T(8,128)}, f32[1]{0:T(128)}, s32[]{:T(128)}, bf16[2,1]{0,1:T(2,128)(2,1)S(1)}, ...), condition=%wide.region_1.2_spmd.clone, body=%wide.region_0.1_spmd.clone.sunk | while | flops 41943044 | bytes 83886232 | solution.py:27
  262.4 0.6 constant_dynamic-slice_fusion.2
  263.6 18.9 %fusion.5 = f32[1024,8192]{1,0:T(8,128)} fusion(f32[1024,8192]{1,0:T(8,128)} %get-tuple-element.204, bf16[2,1024,8192]{2,1,0:T(8,128)(2,1)} %get-tuple-element.216, s32[]{:T(128)} %get-tuple-element.203, f32[]{:T(128)} %bitcast.22, pred[]{:T(512)S(6)} %compare.3, pred[]{:T(512)} %lt.22), kind=kLoop, calls=%fused_computation.1.clone.1 | loop fusion | flops 41943040 | bytes 83886088 | tf_op jit(solution)/shard_map/while/body/eval_jaxpr/jit(_where)/select_n | solution.py:25
  282.4 0.6 constant_dynamic-slice_fusion.2
  283.6 27.0 %fusion.5 = f32[1024,8192]{1,0:T(8,128)} fusion(f32[1024,8192]{1,0:T(8,128)} %get-tuple-element.204, bf16[2,1024,8192]{2,1,0:T(8,128)(2,1)} %get-tuple-element.216, s32[]{:T(128)} %get-tuple-element.203, f32[]{:T(128)} %bitcast.22, pred[]{:T(512)S(6)} %compare.3, pred[]{:T(512)} %lt.22), kind=kLoop, calls=%fused_computation.1.clone.1 | loop fusion | flops 41943040 | bytes 83886088 | tf_op jit(solution)/shard_map/while/body/eval_jaxpr/jit(_where)/select_n | solution.py:25
  310.6 43.1 %add_bitcast_fusion = f32[1,1024,8192]{2,1,0:T(8,128)} fusion(f32[1024,8192]{1,0:T(8,128)} %get-tuple-element.157, f32[1024,8192]{1,0:T(8,128)} %get-tuple-element.115, f32[1024,8192]{1,0:T(8,128)} %param.5, f32[]{:T(128)} %bitcast.3), kind=kLoop, calls=%fused_computation.3 | loop fusion | flops 33554432 | bytes 134217728 | tf_op jit(solution)/shard_map/broadcast_in_dim | solution.py:54
  (3 shorter events, 0.0 us)
Async XLA Ops:
  6.5 181.9 %all-gather.4.cloned.1.call-start = ((), (), s32[]{:S(2)}) async-start(), calls=%async_computation | async-start | bytes 14155776 | tf_op jit(solution)/shard_map/all_gather | solution.py:49
  9.5 203.6 %copy-start = (u32[32]{0:T(128)S(1)}, u32[32]{0:T(128)}, u32[]{:S(2)}) copy-start(u32[32]{0:T(128)} %constant.48) | copy-start | bytes 388
  9.5 252.9 %all-gather.6.cloned.1.call-start = ((), (), s32[]{:S(2)}) async-start(), calls=%async_computation.1 | async-start | bytes 50331648 | tf_op jit(solution)/shard_map/all_gather | solution.py:10
Sparse Core Ops, SparseCore 0:
  9.6 178.8 all-gather.3
  213.2 49.1 all-gather.5
where the time goes:
time: 361 us
  waiting for transfers between devices  225 us (62%)
  other arithmetic  91.9 us (25%)
  matrix products  24.6 us (7%)
  between operations  13.4 us (4%)
    all_gather x1, waiting for transfers between devices, local(): lax.all_gather(scaled, 'assets', axis=1, tiled=True)  179 us
    select_n x2, other arithmetic, turn(): return jax.tree.map(lambda a, b: jnp.where(reached, a, b), new, before)  45.9 us
    all_gather x1, waiting for transfers between devices, prefix(): lax.all_gather(part.astype(kind), axis)  45.6 us
    broadcast_in_dim x1, other arithmetic, local(): return result[None]  43.1 us
    dot_general x1, matrix products, cross_tile(): lax.dot_general(left, right, (((0,), (0,)), ((), ())), preferred_element_...  24.6 us
  transfers between devices with their start and end apart: 2, of which 2 were waited for; matrix products, arithmetic and copies ran while one was open for 0% of the time, Pallas kernels for 0%

commit v1 on v0

--- a/solution.py
+++ b/solution.py
@@ -2,6 +2,12 @@
 import jax.numpy as jnp
 from jax import lax
 from jax.sharding import PartitionSpec as P
+
+
+def all_parts(x, axis, along):
+    pieces = lax.all_gather(x, axis, axis=0, tiled=False)
+    result = jnp.concatenate(pieces, axis=along)
+    return result
 
 
 def prefix(shard, axis, combine, identity):
@@ -46,7 +52,7 @@
     )
     factor = jnp.power(lam, jnp.float32(minutes))
     scaled = (returns.astype(jnp.float32) * weight[:, None]).astype(jnp.bfloat16)
-    tile = cross_tile(scaled, lax.all_gather(scaled, "assets", axis=1, tiled=True))
+    tile = cross_tile(scaled, all_parts(scaled, "assets", 1))
     decay = jnp.full((1,), factor, jnp.float32)
     identity = (jnp.zeros_like(tile), jnp.ones((1,), jnp.float32))
     before, reach = prefix((tile, decay), "tm", combine_carry, identity)

time: 361 us -> 378 us (1.047)
  local copies, waits for them, and re-layouts: 2.47 us -> 19.1 us
    reshape x0 -> x1, local copies, waits for them, and re-layouts: none -> 16.7 us  [all_parts(): result = jnp.concatenate(pieces, axis=along)]
where the time goes in v1:
time: 378 us; the launch traced here: 377 us
  waiting for transfers between devices  225 us (60%)
  other arithmetic  92 us (24%)
  matrix products  24.6 us (7%)
  local copies, waits for them, and re-layouts  19.1 us (5%)
  between operations  13.4 us (4%)
    all_gather x1, waiting for transfers between devices, all_parts(): pieces = lax.all_gather(x, axis, axis=0, tiled=False)  179 us
    select_n x2, other arithmetic, turn(): return jax.tree.map(lambda a, b: jnp.where(reached, a, b), new, before)  45.9 us
    all_gather x1, waiting for transfers between devices, prefix(): lax.all_gather(part.astype(kind), axis)  45.6 us
    broadcast_in_dim x1, other arithmetic, local(): return result[None]  43.1 us
    dot_general x1, matrix products, cross_tile(): lax.dot_general(left, right, (((0,), (0,)), ((), ())), preferred_element_...  24.6 us
    reshape x1, local copies, waits for them, and re-layouts, all_parts(): result = jnp.concatenate(pieces, axis=along)  16.7 us
  transfers between devices with their start and end apart: 2, of which 2 were waited for; matrix products, arithmetic and copies ran while one was open for 0% of the time, Pallas kernels for 0%

profile of v1, /device:TPU:0, one launch (start us, length us, event | category | flops | bytes accessed | tf_op | source)
XLA Modules:
  0.0 377.3 jit_solution(7570115474438580902)
XLA Ops:
  6.5 0.0 all-gather.5.cloned.1.call-start
  6.6 3.0 multiply_convert_fusion
  9.5 0.0 all-gather.5.cloned.1.call-update
  9.5 0.0 all-gather.7.cloned.1.call-start
  9.6 178.9 %all-gather.5.cloned.1.call-done = bf16[6144,1024]{1,0:T(8,128)(2,1)} async-done(((bf16[768,1024]{1,0:T(8,128)(2,1)}), bf16[6144,1024]{1,0:T(8,128)(2,1)}) %all-gather.5.cloned.1.call-update) | async-done | bytes 12582928 | tf_op jit(solution)/shard_map/all_gather | solution.py:8
  188.5 16.7 %copy.5 = bf16[768,8,1024]{0,2,1:T(8,128)(2,1)} copy(bf16[768,8,1024]{2,0,1:T(8,128)(2,1)} %bitcast.30) | data formatting | bytes 25165824 | tf_op jit(solution)/shard_map/reshape | solution.py:9
  205.2 0.0 copy-start
  205.2 24.6 %fusion.1 = (bf16[1024,8192]{1,0:T(8,128)(2,1)}, f32[1024,8192]{1,0:T(8,128)}) fusion(bf16[768,1024]{1,0:T(8,128)(2,1)} %multiply_convert_fusion, bf16[768,8192]{0,1:T(8,128)(2,1)} %bitcast.31), kind=kOutput, calls=%fused_computation.6 | convolution fusion | flops 12893290496 | bytes 64487424 | tf_op jit(solution)/shard_map/dot_general | solution.py:37
  229.7 0.0 all-gather.7.cloned.1.call-update
  229.8 0.0 copy-done
  229.8 0.6 dynamic-slice
  230.4 0.7 dynamic-update-slice
  231.1 2.4 all-reduce
  233.6 45.6 %all-gather.7.cloned.1.call-done = bf16[2048,8192]{1,0:T(8,128)(2,1)} async-done(((bf16[1024,8192]{1,0:T(8,128)(2,1)}), bf16[2048,8192]{1,0:T(8,128)(2,1)}) %all-gather.7.cloned.1.call-update) | async-done | bytes 33554448 | tf_op jit(solution)/shard_map/all_gather | solution.py:16
  279.1 48.2 %while.16 = (s32[]{:T(128)}, f32[1024,8192]{1,0:T(8,128)}, f32[1]{0:T(128)}, s32[]{:T(128)}, bf16[2,1]{0,1:T(2,128)(2,1)S(1)}, /*index=5*/bf16[2,1024,8192]{2,1,0:T(8,128)(2,1)}, s32[]{:T(128)}, s32[]{:T(128)}) while((s32[]{:T(128)}, f32[1024,8192]{1,0:T(8,128)}, f32[1]{0:T(128)}, s32[]{:T(128)}, bf16[2,1]{0,1:T(2,128)(2,1)S(1)}, ...), condition=%wide.region_1.2_spmd.clone, body=%wide.region_0.1_spmd.clone.sunk | while | flops 41943044 | bytes 83886232 | solution.py:33
  279.1 0.6 constant_dynamic-slice_fusion.2
  280.3 18.9 %fusion.5 = f32[1024,8192]{1,0:T(8,128)} fusion(f32[1024,8192]{1,0:T(8,128)} %get-tuple-element.216, bf16[2,1024,8192]{2,1,0:T(8,128)(2,1)} %get-tuple-element.228, s32[]{:T(128)} %get-tuple-element.215, f32[]{:T(128)} %bitcast.26, pred[]{:T(512)S(6)} %compare.3, pred[]{:T(512)} %lt.22), kind=kLoop, calls=%fused_computation.1.clone.1 | loop fusion | flops 41943040 | bytes 83886088 | tf_op jit(solution)/shard_map/while/body/eval_jaxpr/jit(_where)/select_n | solution.py:31
  299.1 0.6 constant_dynamic-slice_fusion.2
  300.3 27.0 %fusion.5 = f32[1024,8192]{1,0:T(8,128)} fusion(f32[1024,8192]{1,0:T(8,128)} %get-tuple-element.216, bf16[2,1024,8192]{2,1,0:T(8,128)(2,1)} %get-tuple-element.228, s32[]{:T(128)} %get-tuple-element.215, f32[]{:T(128)} %bitcast.26, pred[]{:T(512)S(6)} %compare.3, pred[]{:T(512)} %lt.22), kind=kLoop, calls=%fused_computation.1.clone.1 | loop fusion | flops 41943040 | bytes 83886088 | tf_op jit(solution)/shard_map/while/body/eval_jaxpr/jit(_where)/select_n | solution.py:31
  327.3 43.1 %add_bitcast_fusion = f32[1,1024,8192]{2,1,0:T(8,128)} fusion(f32[1024,8192]{1,0:T(8,128)} %get-tuple-element.169, f32[1024,8192]{1,0:T(8,128)} %get-tuple-element.115, f32[1024,8192]{1,0:T(8,128)} %param.5, f32[]{:T(128)} %bitcast.6), kind=kLoop, calls=%fused_computation.3 | loop fusion | flops 33554432 | bytes 134217728 | tf_op jit(solution)/shard_map/broadcast_in_dim | solution.py:60
  (3 shorter events, 0.0 us)
Async XLA Ops:
  6.5 182.0 %all-gather.5.cloned.1.call-start = ((), (), s32[]{:S(2)}) async-start(), calls=%async_computation | async-start | bytes 14155776 | tf_op jit(solution)/shard_map/all_gather | solution.py:8
  9.5 269.6 %all-gather.7.cloned.1.call-start = ((), (), s32[]{:S(2)}) async-start(), calls=%async_computation.1 | async-start | bytes 50331648 | tf_op jit(solution)/shard_map/all_gather | solution.py:16
  205.2 24.6 %copy-start = (u32[32]{0:T(128)S(1)}, u32[32]{0:T(128)}, u32[]{:S(2)}) copy-start(u32[32]{0:T(128)} %constant.48) | copy-start | bytes 388
Sparse Core Ops, SparseCore 0:
  9.7 178.8 all-gather.4
  229.9 49.1 all-gather.6
